TPU v7x, 256 devices: a whole 4x4x8 slice. The times are simulated.
256 devices in a mesh: head: 8 (over z_hi, core), outer: 2 (over z_lo), inner: 16 (over y, x).
Axes of the slice: x: 4, y: 4, z: 8 (z_hi: 4, z_lo: 2; z = z_hi * 2 + z_lo), core: 2. Of those that a mesh axis runs over, the one named last changes fastest.
Arguments:
- query: bfloat16 [32768, 8192], P(('outer', 'inner', 'head')), may hold values from -100 to 100
- keys: bfloat16 [32768, 1024], P(('outer', 'inner', 'head')), may hold values from -4.5 to 4.5
- values: bfloat16 [32768, 1024], P(('outer', 'inner', 'head')), may hold values from -6 to 6
- lengths: int32 [32], replicated, may hold values from 1 to 2048, 32768 in all
Outputs:
- attended: bfloat16 [32768, 8192], P(('outer', 'inner', 'head'))
Inputs may be any that keep to these rules, and one draw needn't show every extreme that they name: `lengths`: they sum to 32768, and the longest is exactly 2048.
All inputs are finite; a program needn't handle non-finite values.
Results may differ from a plain program's by a relative error of at most 0.0038.
Values may be sent and summed in bfloat16 or wider, within the bound.
No kernel may reach another device: no remote copies, remote signals or barrier semaphores. Data moves between devices by JAX's collectives and lax.ppermute only.
A program may use at most 64 MiB of HBM per device.

v0:
```python
import math

import jax
import jax.numpy as jnp
from jax import lax
from jax.sharding import PartitionSpec as P

HEAD_SIZE = 128


def from_behind(value, axis, steps):
    count = lax.axis_size(axis)
    leading, last = (max(0, -steps), min(count, count - steps))
    return lax.ppermute(value, axis, [(source, source + steps) for source in range(leading, last)])


def doc_numbers(lengths, start_pos, count):
    ends = jnp.cumsum(lengths)
    positions = start_pos + lax.iota(jnp.int32, count)
    numbers = jnp.sum((positions[:, None] >= ends[None, :]).astype(jnp.int32), axis=1)
    return (numbers, positions)


def per_device(query, keys, values, lengths):
    query_local, keys_local, values_local = (
        lax.all_to_all(query, "head", split_axis=1, concat_axis=0, tiled=True),
        lax.all_to_all(keys, "head", split_axis=1, concat_axis=0, tiled=True),
        lax.all_to_all(values, "head", split_axis=1, concat_axis=0, tiled=True),
    )
    local_len = query_local.shape[0]
    pair_heads = keys_local.shape[1] // HEAD_SIZE
    group_width = query_local.shape[1] // keys_local.shape[1]
    context_count = lax.axis_size(("outer", "inner"))
    reach_hops = min(2, context_count // 4)
    position_index = lax.axis_index(("outer", "inner"))
    query_docs, query_pos = doc_numbers(lengths, position_index * local_len, local_len)
    query_groups = jnp.transpose(
        query_local.reshape(local_len, pair_heads, group_width, HEAD_SIZE), (2, 0, 1, 3)
    )
    score_scale = 1.0 / math.sqrt(HEAD_SIZE)

    def attend(state, stacked, distance):
        key_heads = stacked[0].reshape(local_len, pair_heads, HEAD_SIZE)
        value_heads = stacked[1].reshape(local_len, pair_heads, HEAD_SIZE)
        key_docs, key_pos = doc_numbers(lengths, (position_index - distance) * local_len, local_len)
        visible = (
            (query_docs[:, None] == key_docs[None, :])
            & (key_pos[None, :] <= query_pos[:, None])
            & (key_pos[None, :] >= 0)
        )

        def one_group(operands):
            query_part, running_max, running_total, running_sum = operands
            scores = (
                jnp.einsum(
                    "qkd,ckd->kqc", query_part, key_heads, preferred_element_type=jnp.float32
                )
                * score_scale
            )
            masked = jnp.where(visible, scores, -1e30)
            new_max = jnp.maximum(running_max, jnp.max(masked, axis=2))
            weights = jnp.where(visible, jnp.exp(masked - new_max[..., None]), 0.0)
            shrink = jnp.exp(running_max - new_max)
            new_total = running_total * shrink + jnp.sum(weights, axis=2)
            update = jnp.einsum(
                "kqc,ckd->qkd",
                weights.astype(jnp.bfloat16),
                value_heads,
                preferred_element_type=jnp.float32,
            )
            new_sum = running_sum * jnp.transpose(shrink, (1, 0))[..., None] + update
            return (new_max, new_total, new_sum)

        return lax.map(one_group, (query_groups, state[0], state[1], state[2]))

    start_state = (
        jnp.full((group_width, pair_heads, local_len), -1e30, jnp.float32),
        jnp.zeros((group_width, pair_heads, local_len), jnp.float32),
        jnp.zeros((group_width, local_len, pair_heads, HEAD_SIZE), jnp.float32),
    )
    own_pair = jnp.stack((keys_local, values_local))
    state = attend(start_state, own_pair, 0)
    carried = own_pair
    for distance in range(1, reach_hops + 1):
        carried = from_behind(carried, ("outer", "inner"), 1)
        state = attend(state, carried, distance)
    running_max, running_total, running_sum = state
    outcome = running_sum / jnp.transpose(running_total, (0, 2, 1))[..., None]
    outcome = jnp.transpose(outcome, (1, 2, 0, 3))
    outcome = outcome.reshape(local_len, pair_heads * group_width * HEAD_SIZE).astype(jnp.bfloat16)
    return lax.all_to_all(outcome, "head", split_axis=0, concat_axis=1, tiled=True)


def solution(mesh):
    placed = (
        P(("outer", "inner", "head"), None),
        P(("outer", "inner", "head"), None),
        P(("outer", "inner", "head"), None),
        P(),
    )
    return jax.shard_map(
        per_device,
        mesh=mesh,
        in_specs=placed,
        out_specs=P(("outer", "inner", "head"), None),
        check_vma=False,
    )
```

profile of v0, /device:TPU:33, one launch (start us, length us, event | category | flops | bytes accessed | tf_op | source)
XLA Modules:
  0.0 369.9 jit_solution(17014296130180950947)
XLA Ops:
  1.8 8.2 %all-to-all-start.1 = ((bf16[128,8,128]{0,2,1:T(8,128)(2,1)}), bf16[128,8,128]{0,2,1:T(8,128)(2,1)S(1)}, u32[]{:S(2)}, u32[]{:S(2)}) async-start(bf16[128,8,128]{0,2,1:T(8,128)(2,1)} %bitcast.2), calls=%async_computation.1 | async-start | bytes 524288 | tf_op jit(solution)/shard_map/all_to_all | solution.py:27
  11.8 8.1 %all-to-all-done.1 = bf16[128,8,128]{0,2,1:T(8,128)(2,1)S(1)} async-done(((bf16[128,8,128]{0,2,1:T(8,128)(2,1)}), bf16[128,8,128]{0,2,1:T(8,128)(2,1)S(1)}, u32[]{:S(2)}, u32[]{:S(2)}) %all-to-all-start.1) | async-done | bytes 262176 | tf_op jit(solution)/shard_map/all_to_all | solution.py:27
  19.9 4.7 %all-to-all-start.2 = ((bf16[128,8,128]{0,2,1:T(8,128)(2,1)}), bf16[128,8,128]{0,2,1:T(8,128)(2,1)S(1)}, u32[]{:S(2)}, u32[]{:S(2)}) async-start(bf16[128,8,128]{0,2,1:T(8,128)(2,1)} %bitcast.5), calls=%async_computation.2 | async-start | bytes 524288 | tf_op jit(solution)/shard_map/all_to_all | solution.py:28
  24.6 3.1 copy.62
  27.7 6.6 %all-to-all-done.2 = bf16[128,8,128]{0,2,1:T(8,128)(2,1)S(1)} async-done(((bf16[128,8,128]{0,2,1:T(8,128)(2,1)}), bf16[128,8,128]{0,2,1:T(8,128)(2,1)S(1)}, u32[]{:S(2)}, u32[]{:S(2)}) %all-to-all-start.2) | async-done | bytes 262176 | tf_op jit(solution)/shard_map/all_to_all | solution.py:28
  34.3 6.5 %all-to-all-start = ((bf16[128,8,1024]{2,0,1:T(8,128)(2,1)}), bf16[128,8,1024]{2,0,1:T(8,128)(2,1)S(1)}, u32[]{:S(2)}, u32[]{:S(2)}) async-start(bf16[128,8,1024]{2,0,1:T(8,128)(2,1)} %bitcast.142), calls=%async_computation | async-start | bytes 4194304 | tf_op jit(solution)/shard_map/all_to_all | solution.py:26
  42.1 3.1 collective-permute-start
  45.2 58.2 %collective-permute-done = bf16[2,1024,128]{2,1,0:T(8,128)(2,1)} collective-permute-done((bf16[2,1024,128]{2,1,0:T(8,128)(2,1)}, bf16[2,1024,128]{2,1,0:T(8,128)(2,1)}, u32[]{:S(2)}, u32[]{:S(2)}) %collective-permute-start) | collective-permute-done | bytes 524320 | tf_op jit(solution)/shard_map/ppermute | solution.py:14
  107.8 15.0 %collective-permute-done.1 = bf16[2,1024,128]{2,1,0:T(8,128)(2,1)} collective-permute-done((bf16[2,1024,128]{2,1,0:T(8,128)(2,1)}, bf16[2,1024,128]{2,1,0:T(8,128)(2,1)}, u32[]{:S(2)}, u32[]{:S(2)}) %collective-permute-start.1) | collective-permute-done | bytes 524320 | tf_op jit(solution)/shard_map/ppermute | solution.py:14
  124.7 2.3 broadcast.193.clone.1
  127.1 53.4 %while.43 = (s32[]{:T(128)}, f32[8,1,1024]{2,1,0:T(1,128)S(1)}, f32[8,1,1024]{2,1,0:T(1,128)S(1)}, f32[8,1024,1,128]{3,1,2,0:T(8,128)}, bf16[8,1024,1,128]{3,1,2...) while((s32[]{:T(128)}, f32[8,1,1024]{2,1,0:T(1,128)S(1)}, ...), condition=%wide.region_5.6_spmd.clone, body=%wide.region_2.0_spmd.clone.sunk | while | flops 563220480 | bytes 13987445 | solution.py:74
  128.6 3.0 fusion.106
  131.5 2.2 fusion.105
  135.2 3.0 fusion.106
  138.2 2.2 fusion.105
  141.9 3.0 fusion.106
  144.9 2.2 fusion.105
  148.6 3.0 fusion.106
  151.6 2.2 fusion.105
  155.3 3.0 fusion.106
  158.2 2.2 fusion.105
  161.9 3.0 fusion.106
  164.9 2.2 fusion.105
  168.6 3.0 fusion.106
  171.6 2.2 fusion.105
  175.3 3.0 fusion.106
  178.3 2.2 fusion.105
  180.5 2.3 broadcast.193.clone
  182.8 61.7 %while.44 = (s32[]{:T(128)}, f32[8,1,1024]{2,1,0:T(1,128)S(1)}, f32[8,1,1024]{2,1,0:T(1,128)S(1)}, f32[8,1024,1,128]{3,1,2,0:T(8,128)}, f32[8,1,1024]{2,1,0:T(1,...) while((s32[]{:T(128)}, f32[8,1,1024]{2,1,0:T(1,128)S(1)}, ...), condition=%wide.region_10.11_spmd.clone, body=%wide.region_7.10_spmd.clone.sunk | while | flops 563351552 | bytes 14540449 | solution.py:74
  184.3 4.0 %fusion.111 = f32[8,1024,1,128]{3,1,2,0:T(8,128)} fusion(f32[8,1024,1,128]{3,1,2,0:T(8,128)} %get-tuple-element.859, s32[]{:T(128)} %get-tuple-element.856, f32[1024,1024]{0,1:T(8,128)S(1)} %get-tuple-element.783, f32[1024]{0:T(1024)S(1)} %get-tuple-element.785, f32[8,1024,1,128]{3,1,2,0:T(8,128)} %get-tuple-element.880, ...), kind=kOutput, calls=%fused_computation.37.clone.1 | convolution fusion | flops 278134784 | bytes 5531136 | tf_op jit(solution)/shard_map/while/body/eval_jaxpr/kqc,ckd->qkd/dot_general | solution.py:65
  188.3 2.2 fusion.110
  192.0 4.0 %fusion.111 = f32[8,1024,1,128]{3,1,2,0:T(8,128)} fusion(f32[8,1024,1,128]{3,1,2,0:T(8,128)} %get-tuple-element.859, s32[]{:T(128)} %get-tuple-element.856, f32[1024,1024]{0,1:T(8,128)S(1)} %get-tuple-element.783, f32[1024]{0:T(1024)S(1)} %get-tuple-element.785, f32[8,1024,1,128]{3,1,2,0:T(8,128)} %get-tuple-element.880, ...), kind=kOutput, calls=%fused_computation.37.clone.1 | convolution fusion | flops 278134784 | bytes 5531136 | tf_op jit(solution)/shard_map/while/body/eval_jaxpr/kqc,ckd->qkd/dot_general | solution.py:65
  196.0 2.2 fusion.110
  199.7 4.0 %fusion.111 = f32[8,1024,1,128]{3,1,2,0:T(8,128)} fusion(f32[8,1024,1,128]{3,1,2,0:T(8,128)} %get-tuple-element.859, s32[]{:T(128)} %get-tuple-element.856, f32[1024,1024]{0,1:T(8,128)S(1)} %get-tuple-element.783, f32[1024]{0:T(1024)S(1)} %get-tuple-element.785, f32[8,1024,1,128]{3,1,2,0:T(8,128)} %get-tuple-element.880, ...), kind=kOutput, calls=%fused_computation.37.clone.1 | convolution fusion | flops 278134784 | bytes 5531136 | tf_op jit(solution)/shard_map/while/body/eval_jaxpr/kqc,ckd->qkd/dot_general | solution.py:65
  203.8 2.2 fusion.110
  207.5 4.0 %fusion.111 = f32[8,1024,1,128]{3,1,2,0:T(8,128)} fusion(f32[8,1024,1,128]{3,1,2,0:T(8,128)} %get-tuple-element.859, s32[]{:T(128)} %get-tuple-element.856, f32[1024,1024]{0,1:T(8,128)S(1)} %get-tuple-element.783, f32[1024]{0:T(1024)S(1)} %get-tuple-element.785, f32[8,1024,1,128]{3,1,2,0:T(8,128)} %get-tuple-element.880, ...), kind=kOutput, calls=%fused_computation.37.clone.1 | convolution fusion | flops 278134784 | bytes 5531136 | tf_op jit(solution)/shard_map/while/body/eval_jaxpr/kqc,ckd->qkd/dot_general | solution.py:65
  211.5 2.2 fusion.110
  215.2 4.0 %fusion.111 = f32[8,1024,1,128]{3,1,2,0:T(8,128)} fusion(f32[8,1024,1,128]{3,1,2,0:T(8,128)} %get-tuple-element.859, s32[]{:T(128)} %get-tuple-element.856, f32[1024,1024]{0,1:T(8,128)S(1)} %get-tuple-element.783, f32[1024]{0:T(1024)S(1)} %get-tuple-element.785, f32[8,1024,1,128]{3,1,2,0:T(8,128)} %get-tuple-element.880, ...), kind=kOutput, calls=%fused_computation.37.clone.1 | convolution fusion | flops 278134784 | bytes 5531136 | tf_op jit(solution)/shard_map/while/body/eval_jaxpr/kqc,ckd->qkd/dot_general | solution.py:65
  219.2 2.2 fusion.110
  222.9 4.0 %fusion.111 = f32[8,1024,1,128]{3,1,2,0:T(8,128)} fusion(f32[8,1024,1,128]{3,1,2,0:T(8,128)} %get-tuple-element.859, s32[]{:T(128)} %get-tuple-element.856, f32[1024,1024]{0,1:T(8,128)S(1)} %get-tuple-element.783, f32[1024]{0:T(1024)S(1)} %get-tuple-element.785, f32[8,1024,1,128]{3,1,2,0:T(8,128)} %get-tuple-element.880, ...), kind=kOutput, calls=%fused_computation.37.clone.1 | convolution fusion | flops 278134784 | bytes 5531136 | tf_op jit(solution)/shard_map/while/body/eval_jaxpr/kqc,ckd->qkd/dot_general | solution.py:65
  226.9 2.2 fusion.110
  230.6 4.0 %fusion.111 = f32[8,1024,1,128]{3,1,2,0:T(8,128)} fusion(f32[8,1024,1,128]{3,1,2,0:T(8,128)} %get-tuple-element.859, s32[]{:T(128)} %get-tuple-element.856, f32[1024,1024]{0,1:T(8,128)S(1)} %get-tuple-element.783, f32[1024]{0:T(1024)S(1)} %get-tuple-element.785, f32[8,1024,1,128]{3,1,2,0:T(8,128)} %get-tuple-element.880, ...), kind=kOutput, calls=%fused_computation.37.clone.1 | convolution fusion | flops 278134784 | bytes 5531136 | tf_op jit(solution)/shard_map/while/body/eval_jaxpr/kqc,ckd->qkd/dot_general | solution.py:65
  234.6 2.2 fusion.110
  238.3 4.0 %fusion.111 = f32[8,1024,1,128]{3,1,2,0:T(8,128)} fusion(f32[8,1024,1,128]{3,1,2,0:T(8,128)} %get-tuple-element.859, s32[]{:T(128)} %get-tuple-element.856, f32[1024,1024]{0,1:T(8,128)S(1)} %get-tuple-element.783, f32[1024]{0:T(1024)S(1)} %get-tuple-element.785, f32[8,1024,1,128]{3,1,2,0:T(8,128)} %get-tuple-element.880, ...), kind=kOutput, calls=%fused_computation.37.clone.1 | convolution fusion | flops 278134784 | bytes 5531136 | tf_op jit(solution)/shard_map/while/body/eval_jaxpr/kqc,ckd->qkd/dot_general | solution.py:65
  242.4 2.2 fusion.110
  244.6 2.3 broadcast.193
  246.9 62.6 %while.45 = (s32[]{:T(128)}, f32[8,1,1024]{2,0,1:T(8,128)S(1)}, f32[8,1024,1,128]{3,1,2,0:T(8,128)}, f32[8,1,1024]{2,1,0:T(1,128)S(1)}, f32[8,1,1024]{2,1,0:T(1,...) while((s32[]{:T(128)}, f32[8,1,1024]{2,0,1:T(8,128)S(1)}, ...), condition=%wide.region_15.16_spmd.clone, body=%wide.region_12.15_spmd.clone.sunk | while | flops 563351552 | bytes 14544549 | solution.py:74
  248.4 4.0 %fusion.116 = f32[8,1024,1,128]{3,1,2,0:T(8,128)} fusion(f32[8,1024,1,128]{3,1,2,0:T(8,128)} %get-tuple-element.906, s32[]{:T(128)} %get-tuple-element.904, f32[1024,1024]{0,1:T(8,128)S(1)} %get-tuple-element.803, f32[1024]{0:T(1024)S(1)} %get-tuple-element.805, f32[8,1024,1,128]{3,1,2,0:T(8,128)} %get-tuple-element.927, ...), kind=kOutput, calls=%fused_computation.62.clone.1 | convolution fusion | flops 278134784 | bytes 5531136 | tf_op jit(solution)/shard_map/while/body/eval_jaxpr/kqc,ckd->qkd/dot_general | solution.py:65
  252.4 2.2 fusion.115
  256.2 4.0 %fusion.116 = f32[8,1024,1,128]{3,1,2,0:T(8,128)} fusion(f32[8,1024,1,128]{3,1,2,0:T(8,128)} %get-tuple-element.906, s32[]{:T(128)} %get-tuple-element.904, f32[1024,1024]{0,1:T(8,128)S(1)} %get-tuple-element.803, f32[1024]{0:T(1024)S(1)} %get-tuple-element.805, f32[8,1024,1,128]{3,1,2,0:T(8,128)} %get-tuple-element.927, ...), kind=kOutput, calls=%fused_computation.62.clone.1 | convolution fusion | flops 278134784 | bytes 5531136 | tf_op jit(solution)/shard_map/while/body/eval_jaxpr/kqc,ckd->qkd/dot_general | solution.py:65
  260.2 2.2 fusion.115
  264.0 4.0 %fusion.116 = f32[8,1024,1,128]{3,1,2,0:T(8,128)} fusion(f32[8,1024,1,128]{3,1,2,0:T(8,128)} %get-tuple-element.906, s32[]{:T(128)} %get-tuple-element.904, f32[1024,1024]{0,1:T(8,128)S(1)} %get-tuple-element.803, f32[1024]{0:T(1024)S(1)} %get-tuple-element.805, f32[8,1024,1,128]{3,1,2,0:T(8,128)} %get-tuple-element.927, ...), kind=kOutput, calls=%fused_computation.62.clone.1 | convolution fusion | flops 278134784 | bytes 5531136 | tf_op jit(solution)/shard_map/while/body/eval_jaxpr/kqc,ckd->qkd/dot_general | solution.py:65
  268.0 2.2 fusion.115
  271.8 4.0 %fusion.116 = f32[8,1024,1,128]{3,1,2,0:T(8,128)} fusion(f32[8,1024,1,128]{3,1,2,0:T(8,128)} %get-tuple-element.906, s32[]{:T(128)} %get-tuple-element.904, f32[1024,1024]{0,1:T(8,128)S(1)} %get-tuple-element.803, f32[1024]{0:T(1024)S(1)} %get-tuple-element.805, f32[8,1024,1,128]{3,1,2,0:T(8,128)} %get-tuple-element.927, ...), kind=kOutput, calls=%fused_computation.62.clone.1 | convolution fusion | flops 278134784 | bytes 5531136 | tf_op jit(solution)/shard_map/while/body/eval_jaxpr/kqc,ckd->qkd/dot_general | solution.py:65
  275.9 2.2 fusion.115
  279.7 4.0 %fusion.116 = f32[8,1024,1,128]{3,1,2,0:T(8,128)} fusion(f32[8,1024,1,128]{3,1,2,0:T(8,128)} %get-tuple-element.906, s32[]{:T(128)} %get-tuple-element.904, f32[1024,1024]{0,1:T(8,128)S(1)} %get-tuple-element.803, f32[1024]{0:T(1024)S(1)} %get-tuple-element.805, f32[8,1024,1,128]{3,1,2,0:T(8,128)} %get-tuple-element.927, ...), kind=kOutput, calls=%fused_computation.62.clone.1 | convolution fusion | flops 278134784 | bytes 5531136 | tf_op jit(solution)/shard_map/while/body/eval_jaxpr/kqc,ckd->qkd/dot_general | solution.py:65
  287.5 4.0 %fusion.116 = f32[8,1024,1,128]{3,1,2,0:T(8,128)} fusion(f32[8,1024,1,128]{3,1,2,0:T(8,128)} %get-tuple-element.906, s32[]{:T(128)} %get-tuple-element.904, f32[1024,1024]{0,1:T(8,128)S(1)} %get-tuple-element.803, f32[1024]{0:T(1024)S(1)} %get-tuple-element.805, f32[8,1024,1,128]{3,1,2,0:T(8,128)} %get-tuple-element.927, ...), kind=kOutput, calls=%fused_computation.62.clone.1 | convolution fusion | flops 278134784 | bytes 5531136 | tf_op jit(solution)/shard_map/while/body/eval_jaxpr/kqc,ckd->qkd/dot_general | solution.py:65
  295.3 4.0 %fusion.116 = f32[8,1024,1,128]{3,1,2,0:T(8,128)} fusion(f32[8,1024,1,128]{3,1,2,0:T(8,128)} %get-tuple-element.906, s32[]{:T(128)} %get-tuple-element.904, f32[1024,1024]{0,1:T(8,128)S(1)} %get-tuple-element.803, f32[1024]{0:T(1024)S(1)} %get-tuple-element.805, f32[8,1024,1,128]{3,1,2,0:T(8,128)} %get-tuple-element.927, ...), kind=kOutput, calls=%fused_computation.62.clone.1 | convolution fusion | flops 278134784 | bytes 5531136 | tf_op jit(solution)/shard_map/while/body/eval_jaxpr/kqc,ckd->qkd/dot_general | solution.py:65
  303.1 4.0 %fusion.116 = f32[8,1024,1,128]{3,1,2,0:T(8,128)} fusion(f32[8,1024,1,128]{3,1,2,0:T(8,128)} %get-tuple-element.906, s32[]{:T(128)} %get-tuple-element.904, f32[1024,1024]{0,1:T(8,128)S(1)} %get-tuple-element.803, f32[1024]{0:T(1024)S(1)} %get-tuple-element.805, f32[8,1024,1,128]{3,1,2,0:T(8,128)} %get-tuple-element.927, ...), kind=kOutput, calls=%fused_computation.62.clone.1 | convolution fusion | flops 278134784 | bytes 5531136 | tf_op jit(solution)/shard_map/while/body/eval_jaxpr/kqc,ckd->qkd/dot_general | solution.py:65
  309.5 2.9 fusion.86
  313.7 2.3 convert_element_type.37
  316.0 47.5 %all_to_all.64 = bf16[8,128,1024]{2,1,0:T(8,128)(2,1)S(1)} all-to-all(bf16[8,128,1024]{2,1,0:T(8,128)(2,1)} %convert_element_type.37), channel_id=1, replica_groups=mesh['head'=8,'outer'=2,'inner'=16] {'head'}, dimensions={0} | all-to-all | bytes 4194304 | tf_op jit(solution)/shard_map/all_to_all | solution.py:91
  363.5 2.4 copy.54
  365.9 4.1 %copy.55 = bf16[128,8192]{1,0:T(8,128)(2,1)} copy(bf16[128,8192]{0,1:T(8,128)(2,1)} %bitcast.198) | data formatting | bytes 4194304 | tf_op jit(solution)/shard_map/all_to_all | solution.py:91
  (133 shorter events, 57.6 us)
Async XLA Ops:
  1.8 18.1 %all-to-all-start.1 = ((bf16[128,8,128]{0,2,1:T(8,128)(2,1)}), bf16[128,8,128]{0,2,1:T(8,128)(2,1)S(1)}, u32[]{:S(2)}, u32[]{:S(2)}) async-start(bf16[128,8,128]{0,2,1:T(8,128)(2,1)} %bitcast.2), calls=%async_computation.1 | async-start | bytes 524288 | tf_op jit(solution)/shard_map/all_to_all | solution.py:27
  19.9 14.4 %all-to-all-start.2 = ((bf16[128,8,128]{0,2,1:T(8,128)(2,1)}), bf16[128,8,128]{0,2,1:T(8,128)(2,1)S(1)}, u32[]{:S(2)}, u32[]{:S(2)}) async-start(bf16[128,8,128]{0,2,1:T(8,128)(2,1)} %bitcast.5), calls=%async_computation.2 | async-start | bytes 524288 | tf_op jit(solution)/shard_map/all_to_all | solution.py:28
  27.7 77.7 %copy-start.2 = (s32[32]{0:T(128)S(1)}, s32[32]{0:T(128)}, u32[]{:S(2)}) copy-start(s32[32]{0:T(128)} %param.13) | copy-start | bytes 388
  34.3 89.5 %all-to-all-start = ((bf16[128,8,1024]{2,0,1:T(8,128)(2,1)}), bf16[128,8,1024]{2,0,1:T(8,128)(2,1)S(1)}, u32[]{:S(2)}, u32[]{:S(2)}) async-start(bf16[128,8,1024]{2,0,1:T(8,128)(2,1)} %bitcast.142), calls=%async_computation | async-start | bytes 4194304 | tf_op jit(solution)/shard_map/all_to_all | solution.py:26
  42.1 61.4 %collective-permute-start = (bf16[2,1024,128]{2,1,0:T(8,128)(2,1)}, bf16[2,1024,128]{2,1,0:T(8,128)(2,1)}, u32[]{:S(2)}, u32[]{:S(2)}) collective-permute-start(bf16[2,1024,128]{2,1,0:T(8,128)(2,1)} %pad_maximum_fusion), channel_id=1, source_target_pairs={{0,1},{1,2},{2,3},{3,4},{4,5},{5,6},{6,7},{7,8},{8,9},{9,10},{10,1... | collective-permute-start | bytes 1572872 | tf_op jit(solution)/shard_map/ppermute | solution.py:14
  103.5 19.3 %collective-permute-start.1 = (bf16[2,1024,128]{2,1,0:T(8,128)(2,1)}, bf16[2,1024,128]{2,1,0:T(8,128)(2,1)}, u32[]{:S(2)}, u32[]{:S(2)}) collective-permute-start(bf16[2,1024,128]{2,1,0:T(8,128)(2,1)} %collective-permute-done), channel_id=1, source_target_pairs={{0,1},{1,2},{2,3},{3,4},{4,5},{5,6},{6,7},{7,8},{8,9},{9,10},{10,1... | collective-permute-start | bytes 1572872 | tf_op jit(solution)/shard_map/ppermute | solution.py:14
  180.5 2.3 copy-start
  180.5 2.3 copy-start.1
where the time goes:
time: 372 us; the launch traced here: 370 us
  matrix products  123 us (33%)
  waiting for transfers between devices  87.9 us (24%)
  other arithmetic  56.9 us (15%)
  blocking collectives  47.5 us (13%)
  local copies, waits for them, and re-layouts  29.1 us (8%)
  starting transfers between devices  24.5 us (7%)
    dot_general x24, matrix products, one_group(): jnp.einsum('kqc,ckd->qkd', weights.astype(jnp.bfloat16), value_heads, pre...  88.2 us
    ppermute x2, waiting for transfers between devices, from_behind(): lax.ppermute(value, axis, [(source, source + steps) for source in range(l...  73.2 us
    reduce_sum x24, other arithmetic, one_group(): new_total = running_total * shrink + jnp.sum(weights, axis=2)  51.9 us
    all_to_all x1, blocking collectives, per_device(): lax.all_to_all(outcome, 'head', split_axis=0, concat_axis=1, tiled=True)  47.5 us
    dot_general x24, matrix products, one_group(): jnp.einsum('qkd,ckd->kqc', query_part, key_heads, preferred_element_type=...  34.6 us
    all_to_all x1, starting transfers between devices, per_device(): lax.all_to_all(keys, 'head', split_axis=1, concat_axis=0, tiled=True)  8.24 us
    all_to_all x1, waiting for transfers between devices, per_device(): lax.all_to_all(keys, 'head', split_axis=1, concat_axis=0, tiled=True)  8.07 us
  transfers between devices with their start and end apart: 5, of which 4 were waited for; matrix products, arithmetic and copies ran while one was open for 3% of the time, Pallas kernels for 0%

commit v1 on v0

v1 whole, which is shorter than its diff:
```python
import functools
import math

import jax
import jax.numpy as jnp
from jax import lax
from jax.experimental import pallas as pl
from jax.experimental.pallas import tpu as pltpu
from jax.sharding import PartitionSpec as P

HD = 128
GW = 8
KVH = 4
TOK = 128
CHIP = 256
ROWS = GW * TOK
RC = 256
SCALE = math.log2(math.e) / math.sqrt(HD)
NEG = -1e30
MESH_AXES = ("head", "outer", "inner")


def attn_kernel(dists, first, last, *refs):
    nk = len(dists)
    sc, q, st = refs[0], refs[1:3], refs[3]
    ks, vs = refs[4 : 4 + 2 * nk : 2], refs[5 : 5 + 2 * nk : 2]
    pos = 4 + 2 * nk
    if not first:
        m_in, l_in, a_in = refs[pos : pos + 3]
        pos += 3
    if last:
        outs = refs[pos : pos + 2]
        pos += 2
    else:
        m_out, l_out, a_out = refs[pos : pos + 3]
        pos += 3
    qs, bias = refs[pos : pos + 2]
    base = sc[1]

    def run(s, masked):
        for h in range(GW):
            qs[h * TOK : (h + 1) * TOK, :] = q[s][:, h * HD : (h + 1) * HD]
        ones = jnp.ones((CHIP, HD), jnp.bfloat16)
        for r0 in range(0, ROWS, RC):
            scores = []
            for j in range(nk):
                x = lax.dot_general(
                    qs[r0 : r0 + RC, :], ks[j][...], (((1,), (1,)), ((), ())),
                    preferred_element_type=jnp.float32,
                )
                if masked:
                    b = bias[s, :, j * CHIP : (j + 1) * CHIP]
                    x = (x.reshape(RC // TOK, TOK, CHIP) + b[None]).reshape(RC, CHIP)
                scores.append(x)
            top = jnp.max(functools.reduce(jnp.maximum, scores), axis=1, keepdims=True)
            rows = pl.ds(s * ROWS + r0, RC)
            if first:
                shift = top * SCALE
            else:
                before = m_in[0, rows, :]
                top = jnp.maximum(before, top)
                shrink = jnp.exp2((before - top) * SCALE)
                shift = top[:, :1] * SCALE
            both = None
            for j in range(nk):
                p = jnp.exp2(scores[j] * SCALE - shift).astype(jnp.bfloat16)
                d = lax.dot_general(
                    p, jnp.concatenate([vs[j][...], ones], axis=1), (((1,), (0,)), ((), ())),
                    preferred_element_type=jnp.float32,
                )
                both = d if both is None else both + d
            a, l = both[:, :HD], both[:, HD:]
            if not first:
                a = a + a_in[0, rows, :] * shrink
                l = l + l_in[0, rows, :] * shrink
            if last:
                o = (a / l).astype(jnp.bfloat16)
                for i in range(RC // TOK):
                    h = r0 // TOK + i
                    outs[s][:, h * HD : (h + 1) * HD] = o[i * TOK : (i + 1) * TOK, :]
            else:
                m_out[0, rows, :] = jnp.broadcast_to(top, (RC, HD))
                l_out[0, rows, :] = l
                a_out[0, rows, :] = a

    def skip(s):
        if last:
            for h in range(GW):
                rows = pl.ds(s * ROWS + h * TOK, TOK)
                outs[s][:, h * HD : (h + 1) * HD] = (a_in[0, rows, :] / l_in[0, rows, :]).astype(
                    jnp.bfloat16
                )
        else:
            rows = pl.ds(s * ROWS, ROWS)
            m_out[0, rows, :] = m_in[0, rows, :]
            l_out[0, rows, :] = l_in[0, rows, :]
            a_out[0, rows, :] = a_in[0, rows, :]

    for s in range(2):

        @pl.when(pl.program_id(0) == 0)
        def _():
            starts = st[s * TOK : (s + 1) * TOK, :1]
            query_pos = base + sc[6 + s] + lax.broadcasted_iota(jnp.int32, (TOK, CHIP), 0)
            for j, d in enumerate(dists):
                key_pos = base - CHIP * d + lax.broadcasted_iota(jnp.int32, (TOK, CHIP), 1)
                visible = key_pos >= starts
                if d == 0:
                    visible = visible & (key_pos <= query_pos)
                bias[s, :, j * CHIP : (j + 1) * CHIP] = jnp.where(visible, 0.0, NEG)

        if first:
            run(s, True)
        else:
            full = functools.reduce(
                jnp.logical_and, [base - CHIP * d >= sc[3 + 2 * s] for d in dists]
            )
            some = functools.reduce(
                jnp.logical_or, [base - CHIP * d + CHIP > sc[2 + 2 * s] for d in dists]
            )
            pl.when(full)(functools.partial(run, s, False))
            pl.when(some & jnp.logical_not(full))(functools.partial(run, s, True))
            pl.when(jnp.logical_not(some))(functools.partial(skip, s))


def attend(sc, query, query_sibling, starts, pairs, dists, state=None, last=False):
    nk, first = len(dists), state is None
    in_specs = [
        pl.BlockSpec((TOK, GW * HD), lambda g, sc: (0, sc[0] * KVH + g)),
        pl.BlockSpec((TOK, GW * HD), lambda g, sc: (0, g)),
        pl.BlockSpec((CHIP, HD), lambda g, sc: (0, 0)),
    ]
    args = [query, query_sibling, starts]
    for pair in pairs:
        in_specs += [
            pl.BlockSpec((CHIP, HD), lambda g, sc: (0, g)),
            pl.BlockSpec((CHIP, HD), lambda g, sc: (0, KVH + g)),
        ]
        args += [pair, pair]
    state_spec = pl.BlockSpec((1, 2 * ROWS, HD), lambda g, sc: (g, 0, 0))
    if not first:
        in_specs += [state_spec] * 3
        args += list(state)
    if last:
        out_shape = [jax.ShapeDtypeStruct((TOK, KVH * GW * HD), jnp.bfloat16)] * 2
        out_specs = [pl.BlockSpec((TOK, GW * HD), lambda g, sc: (0, g))] * 2
    else:
        out_shape = [jax.ShapeDtypeStruct((KVH, 2 * ROWS, HD), jnp.float32)] * 3
        out_specs = [state_spec] * 3
    return pl.pallas_call(
        functools.partial(attn_kernel, tuple(dists), first, last),
        grid_spec=pltpu.PrefetchScalarGridSpec(
            num_scalar_prefetch=1,
            grid=(KVH,),
            in_specs=in_specs,
            out_specs=out_specs,
            scratch_shapes=[
                pltpu.VMEM((ROWS, HD), jnp.bfloat16),
                pltpu.VMEM((2, TOK, nk * CHIP), jnp.float32),
            ],
        ),
        out_shape=out_shape,
        compiler_params=pltpu.CompilerParams(
            dimension_semantics=("arbitrary",), vmem_limit_bytes=32 << 20
        ),
        cost_estimate=pl.CostEstimate(
            flops=KVH * 2 * ROWS * CHIP * nk * HD * 4, bytes_accessed=24 << 20, transcendentals=0
        ),
        name="attend_" + "_".join(str(d) for d in dists),
    )(sc, *args)


def solution(mesh):
    outer, inner, head = (mesh.shape[axis] for axis in ("outer", "inner", "head"))
    devices = outer * inner * head

    def index_of(block):
        return (block % head) * (outer * inner) + block // head

    def behind(value, chips):
        moves = [(index_of(b), index_of((b + 2 * chips) % devices)) for b in range(devices)]
        return lax.ppermute(value, MESH_AXES, moves)

    def swap(value):
        return lax.ppermute(
            value, MESH_AXES, [(index_of(b), index_of(b ^ 1)) for b in range(devices)]
        )

    def per_device(query, keys, values, lengths):
        block = lax.axis_index(("outer", "inner")) * head + lax.axis_index("head")
        core = lax.rem(block, 2)
        base = (block - core) * TOK
        low = core == 0
        half = KVH * HD

        def halves(first_core, second_core):
            return jnp.concatenate([first_core, second_core], axis=1)

        kv_low = halves(keys[:, :half], values[:, :half])
        kv_high = halves(keys[:, half:], values[:, half:])
        kv_mine = jnp.where(low, kv_low, kv_high)
        kv_sibling = swap(jnp.where(low, kv_high, kv_low))
        r0 = jnp.where(
            low,
            jnp.concatenate([kv_mine, kv_sibling], axis=0),
            jnp.concatenate([kv_sibling, kv_mine], axis=0),
        )
        width = KVH * GW * HD
        query_sibling = swap(jnp.where(low, query[:, width:], query[:, :width]))

        order = lax.iota(jnp.int32, lengths.shape[0])
        ends = jnp.sum(jnp.where(order[None, :] <= order[:, None], lengths[None, :], 0), axis=1)

        def start_of(pos):
            return jnp.max(jnp.where(ends[None, :] <= pos[:, None], ends[None, :], 0), axis=1)

        row = lax.iota(jnp.int32, CHIP)
        offset = lax.rem(row + core * TOK, CHIP)
        starts = jnp.broadcast_to(start_of(base + offset)[:, None], (CHIP, HD))
        i8 = lax.iota(jnp.int32, 8)
        pick = jnp.where(i8 == 3, TOK - 1, jnp.where(i8 == 4, TOK, jnp.where(i8 == 5, CHIP - 1, 0)))
        start8 = start_of(base + lax.rem(pick + core * TOK, CHIP))
        sc = jnp.where(
            i8 == 0, core,
            jnp.where(
                i8 == 1, base,
                jnp.where(i8 == 6, core * TOK, jnp.where(i8 == 7, (1 - core) * TOK, start8)),
            ),
        )

        mid = CHIP // 2
        r1, r4, r8 = behind(r0, 1), behind(r0, 4), behind(r0, 8)
        r3 = behind(r4, -1)
        r5 = behind(r1, 4)
        r2a, r2b = behind(r1[:mid], 1), behind(r3[mid:], -1)
        r7 = behind(r3, 4)
        r2 = jnp.concatenate([r2a, r2b], axis=0)
        r6 = behind(r2, 4)

        call = functools.partial(attend, sc, query, query_sibling, starts)
        state = call([r0, r4, r1], (0, 4, 1))
        state = call([r3, r5, r8], (3, 5, 8), state)
        mine, sibling = call([r2, r7, r6], (2, 7, 6), state, True)
        other = swap(sibling)
        return jnp.where(low, halves(mine, other), halves(other, mine))

    tokens = P(("outer", "inner", "head"), None)
    return jax.shard_map(
        per_device,
        mesh=mesh,
        in_specs=(tokens, tokens, tokens, P()),
        out_specs=tokens,
        check_vma=False,
    )
```

time: 372 us -> 159 us (0.43)
  matrix products: 123 us -> 0 us
  other arithmetic: 56.9 us -> 4.37 us
  blocking collectives: 47.5 us -> 0 us
  Pallas kernels: 0 us -> 45.4 us
  waiting for transfers between devices: 87.9 us -> 56.6 us
  local copies, waits for them, and re-layouts: 29.1 us -> 14.7 us
  starting transfers between devices: 24.5 us -> 37.1 us
    dot_general x48 -> x0, matrix products: 123 us -> none  [the longest x24 88.2 us: one_group(): jnp.einsum('kqc,ckd->qkd', weights.astype(jnp.bfloat16), value_heads, pre...]
    reduce_sum x25 -> x1, other arithmetic: 52.1 us -> 0.11 us  [per_device(): jnp.sum(jnp.where(order[None, :] <= order[:, None], lengths[None, :], 0),...]
    all_to_all x1 -> x0, blocking collectives: 47.5 us -> none  [per_device(): lax.all_to_all(outcome, 'head', split_axis=0, concat_axis=1, tiled=True)]
    pallas_call x0 -> x3, Pallas kernels: none -> 45.4 us  [attend(): pl.pallas_call(functools.partial(attn_kernel, tuple(dists), first, last),...]
    ppermute x2 -> x12, starting transfers between devices: 5.02 us -> 37.1 us  [the longest x9 33.5 us: behind(): return lax.ppermute(value, MESH_AXES, moves)]
    all_to_all x3 -> x0, starting transfers between devices: 19.5 us -> none  [the longest x1 8.24 us: per_device(): lax.all_to_all(keys, 'head', split_axis=1, concat_axis=0, tiled=True)]
    ppermute x2 -> x12, waiting for transfers between devices: 73.2 us -> 56.6 us  [the longest x9 53.2 us: behind(): return lax.ppermute(value, MESH_AXES, moves)]
    all_to_all x3 -> x0, waiting for transfers between devices: 14.6 us -> none  [the longest x1 8.07 us: per_device(): lax.all_to_all(keys, 'head', split_axis=1, concat_axis=0, tiled=True)]
  transfers between devices with their start and end apart: 5 -> 12, of which waited for: 4 -> 6; matrix products, arithmetic and copies ran while one was open for 3% -> 2% of each run, Pallas kernels for 0% -> 19%
where the time goes in v1:
time: 159 us; the launch traced here: 158 us
  waiting for transfers between devices  56.6 us (36%)
  Pallas kernels  45.4 us (29%)
  starting transfers between devices  37.1 us (23%)
  local copies, waits for them, and re-layouts  14.7 us (9%)
  other arithmetic  4.37 us (3%)
    ppermute x9, waiting for transfers between devices, behind(): return lax.ppermute(value, MESH_AXES, moves)  53.2 us
    pallas_call x3, Pallas kernels, attend(): pl.pallas_call(functools.partial(attn_kernel, tuple(dists), first, last),...  45.4 us
    ppermute x9, starting transfers between devices, behind(): return lax.ppermute(value, MESH_AXES, moves)  33.5 us
    unnamed x17, local copies, waits for them, and re-layouts  12.3 us
    ppermute x3, starting transfers between devices, swap(): lax.ppermute(value, MESH_AXES, [(index_of(b), index_of(b ^ 1)) for b in r...  3.52 us
    ppermute x3, waiting for transfers between devices, swap(): lax.ppermute(value, MESH_AXES, [(index_of(b), index_of(b ^ 1)) for b in r...  3.45 us
  transfers between devices with their start and end apart: 12, of which 6 were waited for; matrix products, arithmetic and copies ran while one was open for 2% of the time, Pallas kernels for 19%

profile of v1, /device:TPU:33, one launch (start us, length us, event | category | flops | bytes accessed | tf_op | source)
XLA Modules:
  0.0 158.2 jit_solution(6608490782847237527)
XLA Ops:
  0.0 0.0 copy-start
  0.0 0.0 copy-start.7
  0.0 1.3 fusion.5
  1.3 0.1 broadcast_select_fusion.1
  1.4 0.8 collective-permute-start.1
  2.1 1.2 collective-permute-done.1
  3.3 1.0 maximum_select_fusion.1.refs_4_.refs_5_
  4.3 3.0 %collective-permute-start.2 = (bf16[256,1024]{1,0:T(8,128)(2,1)}, bf16[256,1024]{1,0:T(8,128)(2,1)}, u32[]{:S(2)}, u32[]{:S(2)}) collective-permute-start(bf16[256,1024]{1,0:T(8,128)(2,1)} %maximum_select_fusion.1.refs_4_.refs_5_), channel_id=1, source_target_pairs={{0,64},{32,96},{64,128},{96,160},{128,192},{160,224},{192,1},{224,... | collective-permute-start | bytes 1572872 | tf_op jit(solution)/shard_map/ppermute | solution.py:182
  7.3 1.2 collective-permute-start.4
  8.5 0.0 copy-done
  8.5 1.1 slice_select_fusion
  9.6 0.9 collective-permute-start
  10.5 35.8 %collective-permute-done.4.refs_6_.refs_7_ = bf16[256,1024]{1,0:T(8,128)(2,1)} collective-permute-done((bf16[256,1024]{1,0:T(8,128)(2,1)}, bf16[256,1024]{1,0:T(8,128)(2,1)}, u32[]{:S(2)}, u32[]{:S(2)}) %collective-permute-start.4) | collective-permute-done | bytes 524320 | tf_op jit(solution)/shard_map/ppermute | solution.py:182
  46.3 7.8 %collective-permute-start.5 = (bf16[256,1024]{1,0:T(8,128)(2,1)}, bf16[256,1024]{1,0:T(8,128)(2,1)S(1)}, u32[]{:S(2)}, u32[]{:S(2)}) collective-permute-start(bf16[256,1024]{1,0:T(8,128)(2,1)} %collective-permute-done.4.refs_6_.refs_7_), channel_id=1, source_target_pairs={{0,223},{32,255},{64,0},{96,32},{128,64},{160,96},{192,128},{224,1... | collective-permute-start | bytes 1572872 | tf_op jit(solution)/shard_map/ppermute | solution.py:182
  54.1 0.0 copy-done.7
  54.2 0.1 select_reduce_fusion.1
  54.3 0.2 select_reduce_fusion.2
  54.5 0.0 collective-permute-done.2.refs_8_.refs_9_
  54.5 1.0 slice.32
  55.4 1.9 %collective-permute-start.3 = (bf16[128,1024]{1,0:T(8,128)(2,1)S(1)}, bf16[128,1024]{1,0:T(8,128)(2,1)S(1)}, u32[]{:S(2)}, u32[]{:S(2)}) collective-permute-start(bf16[128,1024]{1,0:T(8,128)(2,1)S(1)} %slice.32), channel_id=1, source_target_pairs={{0,64},{32,96},{64,128},{96,160},{128,192},{160,224},{192,1},{224,... | collective-permute-start | bytes 786440 | tf_op jit(solution)/shard_map/ppermute | solution.py:182
  57.3 9.9 %collective-permute-done.5.refs_4_.refs_5_ = bf16[256,1024]{1,0:T(8,128)(2,1)S(1)} collective-permute-done((bf16[256,1024]{1,0:T(8,128)(2,1)}, bf16[256,1024]{1,0:T(8,128)(2,1)S(1)}, u32[]{:S(2)}, u32[]{:S(2)}) %collective-permute-start.5) | collective-permute-done | bytes 524320 | tf_op jit(solution)/shard_map/ppermute | solution.py:182
  67.2 11.3 %collective-permute-start.6 = (bf16[128,1024]{1,0:T(8,128)(2,1)S(1)}, bf16[128,1024]{1,0:T(8,128)(2,1)S(1)}, u32[]{:S(2)}, u32[]{:S(2)}) collective-permute-start(bf16[128,1024]{1,0:T(8,128)(2,1)S(1)} %slice.33), channel_id=1, source_target_pairs={{0,223},{32,255},{64,0},{96,32},{128,64},{160,96},{192,128},{224,1... | collective-permute-start | bytes 786440 | tf_op jit(solution)/shard_map/ppermute | solution.py:182
  78.6 0.1 select_reduce_fusion
  78.6 0.1 collective-permute-start.10
  78.7 3.2 %collective-permute-start.9 = (bf16[256,1024]{1,0:T(8,128)(2,1)}, bf16[256,1024]{1,0:T(8,128)(2,1)S(1)}, u32[]{:S(2)}, u32[]{:S(2)}) collective-permute-start(bf16[256,1024]{1,0:T(8,128)(2,1)} %collective-permute-done.2.refs_8_.refs_9_), channel_id=1, source_target_pairs={{0,1},{32,33},{64,65},{96,97},{128,129},{160,161},{192,193},{224,2... | collective-permute-start | bytes 1572872 | tf_op jit(solution)/shard_map/ppermute | solution.py:182
  82.0 0.0 collective-permute-done.3
  82.0 0.1 collective-permute-start.7
  82.1 0.0 collective-permute-done.6
  82.1 4.9 %collective-permute-start.8 = (bf16[256,1024]{1,0:T(8,128)(2,1)S(1)}, bf16[256,1024]{1,0:T(8,128)(2,1)S(1)}, u32[]{:S(2)}, u32[]{:S(2)}) collective-permute-start(bf16[256,1024]{1,0:T(8,128)(2,1)S(1)} %constant_dynamic-update-slice_fusion.refs_4_.refs_5_), channel_id=1, source_target_pairs={{0,1},{32,33},{64,65},{96,97},{128,129},{160,161},{192,193},{224,2... | collective-permute-start | bytes 1572872 | tf_op jit(solution)/shard_map/ppermute | solution.py:182
  87.0 0.0 collective-permute-done.refs_2_
  87.1 0.1 broadcast_in_dim.84.refs_3_
  87.1 13.6 %attend_0_4_1.1 = (f32[4,2048,128]{2,1,0:T(8,128)S(1)}, f32[4,2048,128]{2,1,0:T(8,128)S(1)}, f32[4,2048,128]{2,1,0:T(8,128)S(1)}) custom-call(s32[8]{0:T(128)S(1)} %compare_select_fusion.10.refs_0_, bf16[128,8192]{1,0:T(8,128)(2,1)S(1)} %copy-done, bf16[128,4096]{1,0:T(8,128)(2,1)S(1)} %collective-permute-done.refs_2_, ...), custom_call_target="tpu_custom_call" | custom-call | flops 3221225472 | bytes 25165824 | tf_op jit(solution)/shard_map/attend_0_4_1/pallas_call | solution.py:150
  100.8 0.0 copy-start.5
  100.8 2.0 %copy-done.5 = f32[4,2048,128]{2,1,0:T(8,128)} copy-done((f32[4,2048,128]{2,1,0:T(8,128)}, f32[4,2048,128]{2,1,0:T(8,128)S(1)}, u32[]{:S(2)}) %copy-start.5) | copy-done | bytes 4194328
  102.7 0.0 copy-start.6
  102.7 2.0 %copy-done.6 = f32[4,2048,128]{2,1,0:T(8,128)} copy-done((f32[4,2048,128]{2,1,0:T(8,128)}, f32[4,2048,128]{2,1,0:T(8,128)S(1)}, u32[]{:S(2)}) %copy-start.6) | copy-done | bytes 4194328
  104.7 0.0 collective-permute-done.10.refs_8_.refs_9_
  104.7 5.1 %collective-permute-done.9.refs_6_.refs_7_ = bf16[256,1024]{1,0:T(8,128)(2,1)S(1)} collective-permute-done((bf16[256,1024]{1,0:T(8,128)(2,1)}, bf16[256,1024]{1,0:T(8,128)(2,1)S(1)}, u32[]{:S(2)}, u32[]{:S(2)}) %collective-permute-start.9) | collective-permute-done | bytes 524320 | tf_op jit(solution)/shard_map/ppermute | solution.py:182
  109.9 16.2 %attend_3_5_8.1 = (f32[4,2048,128]{2,1,0:T(8,128)S(1)}, f32[4,2048,128]{2,1,0:T(8,128)S(1)}, f32[4,2048,128]{2,1,0:T(8,128)S(1)}) custom-call(s32[8]{0:T(128)S(1)} %compare_select_fusion.10.refs_0_, bf16[128,8192]{1,0:T(8,128)(2,1)S(1)} %copy-done, bf16[128,4096]{1,0:T(8,128)(2,1)S(1)} %collective-permute-done.refs_2_, ...), custom_call_target="tpu_custom_call" | custom-call | flops 3221225472 | bytes 25165824 | tf_op jit(solution)/shard_map/attend_3_5_8/pallas_call | solution.py:150
  126.1 0.0 copy-start.1
  126.1 2.0 %copy-done.1 = f32[4,2048,128]{2,1,0:T(8,128)} copy-done((f32[4,2048,128]{2,1,0:T(8,128)}, f32[4,2048,128]{2,1,0:T(8,128)S(1)}, u32[]{:S(2)}) %copy-start.1) | copy-done | bytes 4194328
  128.1 0.0 copy-start.3
  128.1 2.0 %copy-done.3 = f32[4,2048,128]{2,1,0:T(8,128)} copy-done((f32[4,2048,128]{2,1,0:T(8,128)}, f32[4,2048,128]{2,1,0:T(8,128)S(1)}, u32[]{:S(2)}) %copy-start.3) | copy-done | bytes 4194328
  130.0 0.0 collective-permute-done.7.refs_6_.refs_7_
  130.0 2.3 %collective-permute-done.8.refs_8_.refs_9_ = bf16[256,1024]{1,0:T(8,128)(2,1)S(1)} collective-permute-done((bf16[256,1024]{1,0:T(8,128)(2,1)S(1)}, bf16[256,1024]{1,0:T(8,128)(2,1)S(1)}, u32[]{:S(2)}, u32[]{:S(2)}) %collective-permute-start.8) | collective-permute-done | bytes 524320 | tf_op jit(solution)/shard_map/ppermute | solution.py:182
  132.3 0.0 copy-start.2
  132.3 2.2 %copy-done.2 = f32[4,2048,128]{2,1,0:T(8,128)S(1)} copy-done((f32[4,2048,128]{2,1,0:T(8,128)S(1)}, f32[4,2048,128]{2,1,0:T(8,128)}, u32[]{:S(2)}) %copy-start.2) | copy-done | bytes 4194328
  134.5 0.0 copy-start.4
  134.5 2.2 %copy-done.4 = f32[4,2048,128]{2,1,0:T(8,128)S(1)} copy-done((f32[4,2048,128]{2,1,0:T(8,128)S(1)}, f32[4,2048,128]{2,1,0:T(8,128)}, u32[]{:S(2)}) %copy-start.4) | copy-done | bytes 4194328
  136.7 15.6 %attend_2_7_6.1 = (bf16[128,4096]{1,0:T(8,128)(2,1)S(1)}, bf16[128,4096]{1,0:T(8,128)(2,1)S(1)}) custom-call(s32[8]{0:T(128)S(1)} %compare_select_fusion.10.refs_0_, bf16[128,8192]{1,0:T(8,128)(2,1)S(1)} %copy-done, bf16[128,4096]{1,0:T(8,128)(2,1)S(1)} %collective-permute-done.refs_2_, s32[256,128]{1,0:T(8,128)S(1)} %broadcast_in_dim.84.refs_3_, ...), custom_call_target="tpu_custom_call" | custom-call | flops 3221225472 | bytes 25165824 | tf_op jit(solution)/shard_map/attend_2_7_6/pallas_call | solution.py:150
  152.3 1.8 %collective-permute-start.11 = (bf16[128,4096]{1,0:T(8,128)(2,1)S(1)}, bf16[128,4096]{1,0:T(8,128)(2,1)S(1)}, u32[]{:S(2)}, u32[]{:S(2)}) collective-permute-start(bf16[128,4096]{1,0:T(8,128)(2,1)S(1)} %get-tuple-element.20), channel_id=1, source_target_pairs={{0,32},{32,0},{64,96},{96,64},{128,160},{160,128},{192,224},{224,1... | collective-permute-start | bytes 3145736 | tf_op jit(solution)/shard_map/ppermute | solution.py:185
  154.1 2.3 %collective-permute-done.11 = bf16[128,4096]{1,0:T(8,128)(2,1)S(1)} collective-permute-done((bf16[128,4096]{1,0:T(8,128)(2,1)S(1)}, bf16[128,4096]{1,0:T(8,128)(2,1)S(1)}, u32[]{:S(2)}, u32[]{:S(2)}) %collective-permute-start.11) | collective-permute-done | bytes 1048608 | tf_op jit(solution)/shard_map/ppermute | solution.py:185
  156.4 1.8 %maximum_select_fusion = bf16[128,8192]{1,0:T(8,128)(2,1)} fusion(bf16[128,4096]{1,0:T(8,128)(2,1)S(1)} %collective-permute-done.11, bf16[128,4096]{1,0:T(8,128)(2,1)S(1)} %get-tuple-element.19, pred[]{:T(512)S(6)} %eq.36), kind=kLoop, calls=%fused_computation | loop fusion | flops 9437184 | bytes 4194305 | tf_op jit(solution)/shard_map/jit(_where)/select_n | solution.py:245
  (6 shorter events, 0.1 us)
Async XLA Ops:
  0.0 8.5 %copy-start = (bf16[128,8192]{1,0:T(8,128)(2,1)S(1)}, bf16[128,8192]{1,0:T(8,128)(2,1)}, u32[]{:S(2)}) copy-start(bf16[128,8192]{1,0:T(8,128)(2,1)} %refs_1_.5) | copy-start | bytes 6291460
  0.0 54.1 %copy-start.7 = (s32[32]{0:T(128)S(1)}, s32[32]{0:T(128)}, u32[]{:S(2)}) copy-start(s32[32]{0:T(128)} %param.7) | copy-start | bytes 388
  1.4 1.9 %collective-permute-start.1 = (bf16[128,1024]{1,0:T(8,128)(2,1)S(1)}, bf16[128,1024]{1,0:T(8,128)(2,1)S(1)}, u32[]{:S(2)}, u32[]{:S(2)}) collective-permute-start(bf16[128,1024]{1,0:T(8,128)(2,1)S(1)} %get-tuple-element.22), channel_id=1, source_target_pairs={{0,32},{32,0},{64,96},{96,64},{128,160},{160,128},{192,224},{224,1... | collective-permute-start | bytes 786440 | tf_op jit(solution)/shard_map/ppermute | solution.py:185
  4.3 50.2 %collective-permute-start.2 = (bf16[256,1024]{1,0:T(8,128)(2,1)}, bf16[256,1024]{1,0:T(8,128)(2,1)}, u32[]{:S(2)}, u32[]{:S(2)}) collective-permute-start(bf16[256,1024]{1,0:T(8,128)(2,1)} %maximum_select_fusion.1.refs_4_.refs_5_), channel_id=1, source_target_pairs={{0,64},{32,96},{64,128},{96,160},{128,192},{160,224},{192,1},{224,... | collective-permute-start | bytes 1572872 | tf_op jit(solution)/shard_map/ppermute | solution.py:182
  7.3 39.0 %collective-permute-start.4 = (bf16[256,1024]{1,0:T(8,128)(2,1)}, bf16[256,1024]{1,0:T(8,128)(2,1)}, u32[]{:S(2)}, u32[]{:S(2)}) collective-permute-start(bf16[256,1024]{1,0:T(8,128)(2,1)} %maximum_select_fusion.1.refs_4_.refs_5_), channel_id=1, source_target_pairs={{0,1},{32,33},{64,65},{96,97},{128,129},{160,161},{192,193},{224,2... | collective-permute-start | bytes 1572872 | tf_op jit(solution)/shard_map/ppermute | solution.py:182
  9.6 77.5 %collective-permute-start = (bf16[128,4096]{1,0:T(8,128)(2,1)}, bf16[128,4096]{1,0:T(8,128)(2,1)S(1)}, u32[]{:S(2)}, u32[]{:S(2)}) collective-permute-start(bf16[128,4096]{1,0:T(8,128)(2,1)} %slice_select_fusion), channel_id=1, source_target_pairs={{0,32},{32,0},{64,96},{96,64},{128,160},{160,128},{192,224},{224,1... | collective-permute-start | bytes 3145736 | tf_op jit(solution)/shard_map/ppermute | solution.py:185
  46.3 20.9 %collective-permute-start.5 = (bf16[256,1024]{1,0:T(8,128)(2,1)}, bf16[256,1024]{1,0:T(8,128)(2,1)S(1)}, u32[]{:S(2)}, u32[]{:S(2)}) collective-permute-start(bf16[256,1024]{1,0:T(8,128)(2,1)} %collective-permute-done.4.refs_6_.refs_7_), channel_id=1, source_target_pairs={{0,223},{32,255},{64,0},{96,32},{128,64},{160,96},{192,128},{224,1... | collective-permute-start | bytes 1572872 | tf_op jit(solution)/shard_map/ppermute | solution.py:182
  55.4 26.5 %collective-permute-start.3 = (bf16[128,1024]{1,0:T(8,128)(2,1)S(1)}, bf16[128,1024]{1,0:T(8,128)(2,1)S(1)}, u32[]{:S(2)}, u32[]{:S(2)}) collective-permute-start(bf16[128,1024]{1,0:T(8,128)(2,1)S(1)} %slice.32), channel_id=1, source_target_pairs={{0,64},{32,96},{64,128},{96,160},{128,192},{160,224},{192,1},{224,... | collective-permute-start | bytes 786440 | tf_op jit(solution)/shard_map/ppermute | solution.py:182
  67.2 14.9 %collective-permute-start.6 = (bf16[128,1024]{1,0:T(8,128)(2,1)S(1)}, bf16[128,1024]{1,0:T(8,128)(2,1)S(1)}, u32[]{:S(2)}, u32[]{:S(2)}) collective-permute-start(bf16[128,1024]{1,0:T(8,128)(2,1)S(1)} %slice.33), channel_id=1, source_target_pairs={{0,223},{32,255},{64,0},{96,32},{128,64},{160,96},{192,128},{224,1... | collective-permute-start | bytes 786440 | tf_op jit(solution)/shard_map/ppermute | solution.py:182
  78.6 26.1 %collective-permute-start.10 = (bf16[256,1024]{1,0:T(8,128)(2,1)}, bf16[256,1024]{1,0:T(8,128)(2,1)S(1)}, u32[]{:S(2)}, u32[]{:S(2)}) collective-permute-start(bf16[256,1024]{1,0:T(8,128)(2,1)} %maximum_select_fusion.1.refs_4_.refs_5_), channel_id=1, source_target_pairs={{0,2},{32,34},{64,66},{96,98},{128,130},{160,162},{192,194},{224,2... | collective-permute-start | bytes 1572872 | tf_op jit(solution)/shard_map/ppermute | solution.py:182
  78.7 31.1 %collective-permute-start.9 = (bf16[256,1024]{1,0:T(8,128)(2,1)}, bf16[256,1024]{1,0:T(8,128)(2,1)S(1)}, u32[]{:S(2)}, u32[]{:S(2)}) collective-permute-start(bf16[256,1024]{1,0:T(8,128)(2,1)} %collective-permute-done.2.refs_8_.refs_9_), channel_id=1, source_target_pairs={{0,1},{32,33},{64,65},{96,97},{128,129},{160,161},{192,193},{224,2... | collective-permute-start | bytes 1572872 | tf_op jit(solution)/shard_map/ppermute | solution.py:182
  82.0 48.0 %collective-permute-start.7 = (bf16[256,1024]{1,0:T(8,128)(2,1)S(1)}, bf16[256,1024]{1,0:T(8,128)(2,1)S(1)}, u32[]{:S(2)}, u32[]{:S(2)}) collective-permute-start(bf16[256,1024]{1,0:T(8,128)(2,1)S(1)} %collective-permute-done.5.refs_4_.refs_5_), channel_id=1, source_target_pairs={{0,1},{32,33},{64,65},{96,97},{128,129},{160,161},{192,193},{224,2... | collective-permute-start | bytes 1572872 | tf_op jit(solution)/shard_map/ppermute | solution.py:182
  82.1 50.2 %collective-permute-start.8 = (bf16[256,1024]{1,0:T(8,128)(2,1)S(1)}, bf16[256,1024]{1,0:T(8,128)(2,1)S(1)}, u32[]{:S(2)}, u32[]{:S(2)}) collective-permute-start(bf16[256,1024]{1,0:T(8,128)(2,1)S(1)} %constant_dynamic-update-slice_fusion.refs_4_.refs_5_), channel_id=1, source_target_pairs={{0,1},{32,33},{64,65},{96,97},{128,129},{160,161},{192,193},{224,2... | collective-permute-start | bytes 1572872 | tf_op jit(solution)/shard_map/ppermute | solution.py:182
  100.8 2.0 %copy-start.5 = (f32[4,2048,128]{2,1,0:T(8,128)}, f32[4,2048,128]{2,1,0:T(8,128)S(1)}, u32[]{:S(2)}) copy-start(f32[4,2048,128]{2,1,0:T(8,128)S(1)} %get-tuple-element.14.refs_11_) | copy-start | bytes 12582916
  102.7 2.0 %copy-start.6 = (f32[4,2048,128]{2,1,0:T(8,128)}, f32[4,2048,128]{2,1,0:T(8,128)S(1)}, u32[]{:S(2)}) copy-start(f32[4,2048,128]{2,1,0:T(8,128)S(1)} %get-tuple-element.15.refs_12_) | copy-start | bytes 12582916
  126.1 2.0 %copy-start.1 = (f32[4,2048,128]{2,1,0:T(8,128)}, f32[4,2048,128]{2,1,0:T(8,128)S(1)}, u32[]{:S(2)}) copy-start(f32[4,2048,128]{2,1,0:T(8,128)S(1)} %get-tuple-element.17.refs_11_) | copy-start | bytes 12582916
  128.1 2.0 %copy-start.3 = (f32[4,2048,128]{2,1,0:T(8,128)}, f32[4,2048,128]{2,1,0:T(8,128)S(1)}, u32[]{:S(2)}) copy-start(f32[4,2048,128]{2,1,0:T(8,128)S(1)} %get-tuple-element.18.refs_12_) | copy-start | bytes 12582916
  132.3 2.2 %copy-start.2 = (f32[4,2048,128]{2,1,0:T(8,128)S(1)}, f32[4,2048,128]{2,1,0:T(8,128)}, u32[]{:S(2)}) copy-start(f32[4,2048,128]{2,1,0:T(8,128)} %copy-done.1) | copy-start | bytes 12582916
  134.5 2.2 %copy-start.4 = (f32[4,2048,128]{2,1,0:T(8,128)S(1)}, f32[4,2048,128]{2,1,0:T(8,128)}, u32[]{:S(2)}) copy-start(f32[4,2048,128]{2,1,0:T(8,128)} %copy-done.3) | copy-start | bytes 12582916
  152.3 4.1 %collective-permute-start.11 = (bf16[128,4096]{1,0:T(8,128)(2,1)S(1)}, bf16[128,4096]{1,0:T(8,128)(2,1)S(1)}, u32[]{:S(2)}, u32[]{:S(2)}) collective-permute-start(bf16[128,4096]{1,0:T(8,128)(2,1)S(1)} %get-tuple-element.20), channel_id=1, source_target_pairs={{0,32},{32,0},{64,96},{96,64},{128,160},{160,128},{192,224},{224,1... | collective-permute-start | bytes 3145736 | tf_op jit(solution)/shard_map/ppermute | solution.py:185

commit v2 on v1

v2 whole, which is shorter than its diff:
```python
import functools
import math

import jax
import jax.numpy as jnp
from jax import lax
from jax.experimental import pallas as pl
from jax.experimental.pallas import tpu as pltpu
from jax.sharding import PartitionSpec as P

HD = 128
GW = 8
KVH = 4
TOK = 128
CHIP = 256
ROWS = GW * TOK
RC = 256
SCALE = math.log2(math.e) / math.sqrt(HD)
NEG = -1e30
MESH_AXES = ("head", "outer", "inner")
VMEM = pltpu.VMEM


def attn_kernel(dists, first, last, *refs):
    nk = len(dists)
    sc, query, query_sibling, st = refs[:4]
    pairs = refs[4 : 4 + nk]
    pos = 4 + nk
    if not first:
        m_in, l_in, a_in = refs[pos : pos + 3]
        pos += 3
    if last:
        outs = refs[pos : pos + 2]
        pos += 2
    else:
        m_out, l_out, a_out = refs[pos : pos + 3]
        pos += 3
    bias, qs = refs[pos : pos + 2]
    base = sc[1]

    def lanes(start, offset=0):
        return pl.ds(pl.multiple_of(start, HD) + offset, HD)

    def run(s, masked):
        @pl.loop(0, KVH)
        def _(g):
            source = (query, query_sibling)[s]
            shift = sc[0] * (KVH * GW * HD) if s == 0 else 0
            for h in range(GW):
                qs[h * TOK : (h + 1) * TOK, :] = source[:, lanes(shift + g * (GW * HD) + h * HD)]
            ones = jnp.ones((CHIP, HD), jnp.bfloat16)
            ks = [p[:, lanes(g * HD)] for p in pairs]
            vs = [jnp.concatenate([p[:, lanes((KVH + g) * HD)], ones], axis=1) for p in pairs]
            for r0 in range(0, ROWS, RC):
                scores = []
                for j in range(nk):
                    x = lax.dot_general(
                        qs[r0 : r0 + RC, :], ks[j], (((1,), (1,)), ((), ())),
                        preferred_element_type=jnp.float32,
                    )
                    if masked:
                        b = bias[s, :, j * CHIP : (j + 1) * CHIP]
                        x = (x.reshape(RC // TOK, TOK, CHIP) + b[None]).reshape(RC, CHIP)
                    scores.append(x)
                top = jnp.max(functools.reduce(jnp.maximum, scores), axis=1, keepdims=True)
                top = jnp.broadcast_to(top * SCALE, (RC, HD))
                rows = pl.ds(pl.multiple_of((g * 2 + s) * ROWS, ROWS) + r0, RC)
                if not first:
                    before = m_in[rows, :]
                    top = jnp.maximum(before, top)
                    shrink = jnp.exp2(before - top)
                tops = jnp.concatenate([top, top], axis=1)
                both = None
                for j in range(nk):
                    p = jnp.exp2(scores[j] * SCALE - tops).astype(jnp.bfloat16)
                    d = lax.dot_general(
                        p, vs[j], (((1,), (0,)), ((), ())), preferred_element_type=jnp.float32
                    )
                    both = d if both is None else both + d
                a, l = both[:, :HD], both[:, HD:]
                if not first:
                    a = a + a_in[rows, :] * shrink
                    l = l + l_in[rows, :] * shrink
                if last:
                    o = (a / l).astype(jnp.bfloat16)
                    for i in range(RC // TOK):
                        outs[s][:, lanes(g * (GW * HD), r0 // TOK * HD + i * HD)] = o[
                            i * TOK : (i + 1) * TOK, :
                        ]
                else:
                    m_out[rows, :] = top
                    l_out[rows, :] = l
                    a_out[rows, :] = a

    def finish(s):
        @pl.loop(0, KVH)
        def _(g):
            for h in range(GW):
                rows = pl.ds(pl.multiple_of((g * 2 + s) * ROWS, ROWS) + h * TOK, TOK)
                outs[s][:, lanes(g * (GW * HD), h * HD)] = (a_in[rows, :] / l_in[rows, :]).astype(
                    jnp.bfloat16
                )

    for s in range(2):
        starts = st[s * TOK : (s + 1) * TOK, :1]
        query_pos = base + sc[6 + s] + lax.broadcasted_iota(jnp.int32, (TOK, CHIP), 0)
        for j, d in enumerate(dists):
            key_pos = base - CHIP * d + lax.broadcasted_iota(jnp.int32, (TOK, CHIP), 1)
            visible = key_pos >= starts
            if d == 0:
                visible = visible & (key_pos <= query_pos)
            bias[s, :, j * CHIP : (j + 1) * CHIP] = jnp.where(visible, 0.0, NEG)
        if first:
            run(s, True)
        else:
            full = functools.reduce(
                jnp.logical_and, [base - CHIP * d >= sc[3 + 2 * s] for d in dists]
            )
            some = functools.reduce(
                jnp.logical_or, [base - CHIP * d + CHIP > sc[2 + 2 * s] for d in dists]
            )
            pl.when(full)(functools.partial(run, s, False))
            pl.when(some & jnp.logical_not(full))(functools.partial(run, s, True))
            if last:
                pl.when(jnp.logical_not(some))(functools.partial(finish, s))


def attend(sc, query, query_sibling, starts, pairs, dists, state=None, last=False):
    nk, first = len(dists), state is None
    whole = pl.BlockSpec(memory_space=VMEM)
    in_specs = [pl.BlockSpec(memory_space=pltpu.SMEM)] + [whole] * (3 + nk)
    args = [sc, query, query_sibling, starts, *pairs]
    aliases = {}
    if not first:
        if not last:
            aliases = {len(args) + i: i for i in range(3)}
        in_specs += [whole] * 3
        args += [pltpu.with_memory_space_constraint(x, VMEM) for x in state]
    if last:
        out_shape = [jax.ShapeDtypeStruct((TOK, KVH * GW * HD), jnp.bfloat16)] * 2
    else:
        out_shape = [VMEM((KVH * 2 * ROWS, HD), jnp.float32)] * 3
    return pl.pallas_call(
        functools.partial(attn_kernel, tuple(dists), first, last),
        in_specs=in_specs,
        out_specs=[whole] * len(out_shape),
        out_shape=out_shape,
        scratch_shapes=[VMEM((2, TOK, nk * CHIP), jnp.float32), VMEM((ROWS, HD), jnp.bfloat16)],
        input_output_aliases=aliases,
        compiler_params=pltpu.CompilerParams(vmem_limit_bytes=30 << 20),
        cost_estimate=pl.CostEstimate(
            flops=KVH * 2 * ROWS * CHIP * nk * HD * 4, bytes_accessed=4 << 20, transcendentals=0
        ),
        name="attend_" + "_".join(str(d) for d in dists),
    )(*args)


def solution(mesh):
    outer, inner, head = (mesh.shape[axis] for axis in ("outer", "inner", "head"))
    devices = outer * inner * head

    def index_of(block):
        return (block % head) * (outer * inner) + block // head

    def behind(value, chips):
        moves = [(index_of(b), index_of((b + 2 * chips) % devices)) for b in range(devices)]
        return lax.ppermute(value, MESH_AXES, moves)

    def swap(value):
        return lax.ppermute(
            value, MESH_AXES, [(index_of(b), index_of(b ^ 1)) for b in range(devices)]
        )

    def after(value, state):
        value, top = lax.optimization_barrier((value, state[0]))
        return value, [top, *state[1:]]

    def per_device(query, keys, values, lengths):
        block = lax.axis_index(("outer", "inner")) * head + lax.axis_index("head")
        core = lax.rem(block, 2)
        base = (block - core) * TOK
        low = core == 0
        half = KVH * HD

        def halves(first_core, second_core):
            return jnp.concatenate([first_core, second_core], axis=1)

        kv_low = halves(keys[:, :half], values[:, :half])
        kv_high = halves(keys[:, half:], values[:, half:])
        kv_mine = jnp.where(low, kv_low, kv_high)
        kv_sibling = swap(jnp.where(low, kv_high, kv_low))
        r0 = jnp.where(
            low,
            jnp.concatenate([kv_mine, kv_sibling], axis=0),
            jnp.concatenate([kv_sibling, kv_mine], axis=0),
        )
        width = KVH * GW * HD
        query_sibling = swap(jnp.where(low, query[:, width:], query[:, :width]))

        order = lax.iota(jnp.int32, lengths.shape[0])
        ends = jnp.sum(jnp.where(order[None, :] <= order[:, None], lengths[None, :], 0), axis=1)

        def start_of(pos):
            return jnp.max(jnp.where(ends[None, :] <= pos[:, None], ends[None, :], 0), axis=1)

        row = lax.iota(jnp.int32, CHIP)
        offset = lax.rem(row + core * TOK, CHIP)
        starts = jnp.broadcast_to(start_of(base + offset)[:, None], (CHIP, HD))
        i8 = lax.iota(jnp.int32, 8)
        pick = jnp.where(i8 == 3, TOK - 1, jnp.where(i8 == 4, TOK, jnp.where(i8 == 5, CHIP - 1, 0)))
        start8 = start_of(base + lax.rem(pick + core * TOK, CHIP))
        sc = jnp.where(
            i8 == 0, core,
            jnp.where(
                i8 == 1, base,
                jnp.where(i8 == 6, core * TOK, jnp.where(i8 == 7, (1 - core) * TOK, start8)),
            ),
        )

        call = functools.partial(attend, sc, query, query_sibling, starts)
        r4, r1 = behind(r0, 4), behind(r0, 1)
        r3, r8 = behind(r4, -1), behind(r0, 8)
        state = call([r0, r4], (0, 4))
        r1, state = after(r1, state)
        r2, r5 = behind(r1, 1), behind(r1, 4)
        state = call([r1, r8], (1, 8), state)
        r3, state = after(r3, state)
        r7 = behind(r3, 4)
        state = call([r3, r5], (3, 5), state)
        r2, state = after(r2, state)
        r6 = behind(r2, 4)
        state = call([r2, r7], (2, 7), state)
        mine, sibling = call([r6], (6,), state, True)
        other = swap(sibling)
        return jnp.where(low, halves(mine, other), halves(other, mine))

    tokens = P(("outer", "inner", "head"), None)
    return jax.shard_map(
        per_device,
        mesh=mesh,
        in_specs=(tokens, tokens, tokens, P()),
        out_specs=tokens,
        check_vma=False,
    )
```

time: 159 us -> 140 us (0.88)
  waiting for transfers between devices: 56.6 us -> 74.1 us
  Pallas kernels: 45.4 us -> 30.5 us
  local copies, waits for them, and re-layouts: 14.7 us -> 1.22 us
  starting transfers between devices: 37.1 us -> 26.7 us
  other arithmetic: 4.37 us -> 7.03 us
    ppermute x9 -> x8, waiting for transfers between devices: 53.2 us -> 70.1 us  [behind(): return lax.ppermute(value, MESH_AXES, moves)]
    pallas_call x3 -> x5, Pallas kernels: 45.4 us -> 30.5 us  [attend(): pl.pallas_call(functools.partial(attn_kernel, tuple(dists), first, last),...]
    unnamed x17 -> x4, local copies, waits for them, and re-layouts: 12.3 us -> 0.01 us
    ppermute x9 -> x8, starting transfers between devices: 33.5 us -> 24.1 us  [behind(): return lax.ppermute(value, MESH_AXES, moves)]
    select_n x1, other arithmetic: 1.08 us -> 2.78 us  [per_device(): query_sibling = swap(jnp.where(low, query[:, width:], query[:, :width]))]
  transfers between devices with their start and end apart: 12 -> 11, of which waited for: 6 -> 8; matrix products, arithmetic and copies ran while one was open for 2% -> 3% of each run, Pallas kernels for 19% -> 21%
where the time goes in v2:
time: 140 us
  waiting for transfers between devices  74.1 us (53%)
  Pallas kernels  30.5 us (22%)
  starting transfers between devices  26.7 us (19%)
  other arithmetic  7.03 us (5%)
    ppermute x8, waiting for transfers between devices, behind(): return lax.ppermute(value, MESH_AXES, moves)  70.1 us
    pallas_call x5, Pallas kernels, attend(): pl.pallas_call(functools.partial(attn_kernel, tuple(dists), first, last),...  30.5 us
    ppermute x8, starting transfers between devices, behind(): return lax.ppermute(value, MESH_AXES, moves)  24.1 us
    ppermute x3, waiting for transfers between devices, swap(): lax.ppermute(value, MESH_AXES, [(index_of(b), index_of(b ^ 1)) for b in r...  4.03 us
  transfers between devices with their start and end apart: 11, of which 8 were waited for; matrix products, arithmetic and copies ran while one was open for 3% of the time, Pallas kernels for 21%

profile of v2, /device:TPU:33, one launch (start us, length us, event | category | flops | bytes accessed | tf_op | source)
XLA Modules:
  0.0 139.6 jit_solution(18250202125431667235)
XLA Ops:
  0.0 0.0 copy-start
  0.0 0.0 copy-start.1
  0.0 2.8 %slice_select_fusion = bf16[128,4096]{1,0:T(8,128)(2,1)} fusion(bf16[128,8192]{1,0:T(8,128)(2,1)} %refs_1_.9, pred[]{:T(512)S(6)} %eq.36), kind=kLoop, calls=%fused_computation.1 | loop fusion | flops 524288 | bytes 3145729 | tf_op jit(solution)/shard_map/jit(_where)/select_n | solution.py:198
  2.8 0.7 collective-permute-start
  3.5 1.1 fusion.5
  4.6 0.8 broadcast_select_fusion.1
  5.4 0.0 collective-permute-start.1
  5.4 0.0 copy-done.1
  5.4 0.1 select_reduce_fusion.1
  5.5 1.7 %collective-permute-done.1 = bf16[128,1024]{1,0:T(8,128)(2,1)} collective-permute-done((bf16[128,1024]{1,0:T(8,128)(2,1)}, bf16[128,1024]{1,0:T(8,128)(2,1)}, u32[]{:S(2)}, u32[]{:S(2)}) %collective-permute-start.1) | collective-permute-done | bytes 262176 | tf_op jit(solution)/shard_map/ppermute | solution.py:170
  7.3 1.2 maximum_select_fusion.1.refs_4_
  8.5 1.3 collective-permute-start.3
  9.8 0.2 select_reduce_fusion.2
  10.0 3.1 %collective-permute-start.2 = (bf16[256,1024]{1,0:T(8,128)(2,1)S(1)}, bf16[256,1024]{1,0:T(8,128)(2,1)S(1)}, u32[]{:S(2)}, u32[]{:S(2)}) collective-permute-start(bf16[256,1024]{1,0:T(8,128)(2,1)S(1)} %maximum_select_fusion.1.refs_4_), channel_id=1, source_target_pairs={{0,64},{32,96},{64,128},{96,160},{128,192},{160,224},{192,1},{224,... | collective-permute-start | bytes 1572872 | tf_op jit(solution)/shard_map/ppermute | solution.py:167
  13.1 2.5 %collective-permute-start.6 = (bf16[256,1024]{1,0:T(8,128)(2,1)S(1)}, bf16[256,1024]{1,0:T(8,128)(2,1)S(1)}, u32[]{:S(2)}, u32[]{:S(2)}) collective-permute-start(bf16[256,1024]{1,0:T(8,128)(2,1)S(1)} %maximum_select_fusion.1.refs_4_), channel_id=1, source_target_pairs={{0,2},{32,34},{64,66},{96,98},{128,130},{160,162},{192,194},{224,2... | collective-permute-start | bytes 1572872 | tf_op jit(solution)/shard_map/ppermute | solution.py:167
  15.5 0.1 select_reduce_fusion
  15.6 10.5 %collective-permute-done.3.refs_5_ = bf16[256,1024]{1,0:T(8,128)(2,1)S(1)} collective-permute-done((bf16[256,1024]{1,0:T(8,128)(2,1)S(1)}, bf16[256,1024]{1,0:T(8,128)(2,1)S(1)}, u32[]{:S(2)}, u32[]{:S(2)}) %collective-permute-start.3) | collective-permute-done | bytes 524320 | tf_op jit(solution)/shard_map/ppermute | solution.py:167
  26.2 17.2 %collective-permute-start.5 = (bf16[256,1024]{1,0:T(8,128)(2,1)S(1)}, bf16[256,1024]{1,0:T(8,128)(2,1)S(1)}, u32[]{:S(2)}, u32[]{:S(2)}) collective-permute-start(bf16[256,1024]{1,0:T(8,128)(2,1)S(1)} %collective-permute-done.3.refs_5_), channel_id=1, source_target_pairs={{0,223},{32,255},{64,0},{96,32},{128,64},{160,96},{192,128},{224,1... | collective-permute-start | bytes 1572872 | tf_op jit(solution)/shard_map/ppermute | solution.py:167
  43.4 0.0 collective-permute-done.refs_2_
  43.4 0.1 broadcast_in_dim.84.refs_3_
  43.5 0.0 copy-done
  43.5 8.9 %attend_0_4.1 = (f32[8192,128]{1,0:T(8,128)S(1)}, f32[8192,128]{1,0:T(8,128)S(1)}, f32[8192,128]{1,0:T(8,128)S(1)}) custom-call(s32[8]{0:T(128)S(1)} %compare_select_fusion.10.refs_0_, bf16[128,8192]{1,0:T(8,128)(2,1)S(1)} %copy-done, bf16[128,4096]{1,0:T(8,128)(2,1)S(1)} %collective-permute-done.refs_2_, s32[256,128]{1,0:T(8,128)S(1)} %broadcast_in_dim.84.refs_3_, ...), custom_call_target="tpu_custom_call" | custom-call | flops 2147483648 | bytes 4194304 | tf_op jit(solution)/shard_map/attend_0_4/pallas_call | solution.py:143
  52.4 18.0 %collective-permute-done.2.refs_4_ = bf16[256,1024]{1,0:T(8,128)(2,1)S(1)} collective-permute-done((bf16[256,1024]{1,0:T(8,128)(2,1)S(1)}, bf16[256,1024]{1,0:T(8,128)(2,1)S(1)}, u32[]{:S(2)}, u32[]{:S(2)}) %collective-permute-start.2) | collective-permute-done | bytes 524320 | tf_op jit(solution)/shard_map/ppermute | solution.py:167
  70.4 0.0 collective-permute-start.7
  70.4 0.0 collective-permute-start.4
  70.4 0.0 collective-permute-done.6.refs_5_
  70.4 9.8 %attend_1_8.1 = (f32[8192,128]{1,0:T(8,128)S(1)}, f32[8192,128]{1,0:T(8,128)S(1)}, f32[8192,128]{1,0:T(8,128)S(1)}) custom-call(s32[8]{0:T(128)S(1)} %compare_select_fusion.10.refs_0_, bf16[128,8192]{1,0:T(8,128)(2,1)S(1)} %copy-done, bf16[128,4096]{1,0:T(8,128)(2,1)S(1)} %collective-permute-done.refs_2_, ...), custom_call_target="tpu_custom_call", output_to_operand_aliasing={{0}: (6, {}), {1}: (7, {}), {2}: (8, {})} | custom-call | flops 2147483648 | bytes 4194304 | tf_op jit(solution)/shard_map/attend_1_8/pallas_call | solution.py:143
  80.2 0.0 collective-permute-done.5.refs_4_
  80.2 0.1 collective-permute-start.9
  80.3 6.9 %collective-permute-done.7.refs_5_ = bf16[256,1024]{1,0:T(8,128)(2,1)S(1)} collective-permute-done((bf16[256,1024]{1,0:T(8,128)(2,1)S(1)}, bf16[256,1024]{1,0:T(8,128)(2,1)S(1)}, u32[]{:S(2)}, u32[]{:S(2)}) %collective-permute-start.7) | collective-permute-done | bytes 524320 | tf_op jit(solution)/shard_map/ppermute | solution.py:167
  87.2 0.7 attend_3_5.1
  87.9 26.1 %collective-permute-done.4.refs_4_ = bf16[256,1024]{1,0:T(8,128)(2,1)S(1)} collective-permute-done((bf16[256,1024]{1,0:T(8,128)(2,1)S(1)}, bf16[256,1024]{1,0:T(8,128)(2,1)S(1)}, u32[]{:S(2)}, u32[]{:S(2)}) %collective-permute-start.4) | collective-permute-done | bytes 524320 | tf_op jit(solution)/shard_map/ppermute | solution.py:167
  113.9 0.0 collective-permute-start.8
  113.9 6.3 %collective-permute-done.9.refs_5_ = bf16[256,1024]{1,0:T(8,128)(2,1)S(1)} collective-permute-done((bf16[256,1024]{1,0:T(8,128)(2,1)S(1)}, bf16[256,1024]{1,0:T(8,128)(2,1)S(1)}, u32[]{:S(2)}, u32[]{:S(2)}) %collective-permute-start.9) | collective-permute-done | bytes 524320 | tf_op jit(solution)/shard_map/ppermute | solution.py:167
  120.2 9.6 %attend_2_7.1 = (f32[8192,128]{1,0:T(8,128)S(1)}, f32[8192,128]{1,0:T(8,128)S(1)}, f32[8192,128]{1,0:T(8,128)S(1)}) custom-call(s32[8]{0:T(128)S(1)} %compare_select_fusion.10.refs_0_, bf16[128,8192]{1,0:T(8,128)(2,1)S(1)} %copy-done, bf16[128,4096]{1,0:T(8,128)(2,1)S(1)} %collective-permute-done.refs_2_, ...), custom_call_target="tpu_custom_call", output_to_operand_aliasing={{0}: (6, {}), {1}: (7, {}), {2}: (8, {})} | custom-call | flops 2147483648 | bytes 4194304 | tf_op jit(solution)/shard_map/attend_2_7/pallas_call | solution.py:143
  129.8 2.3 %collective-permute-done.8.refs_4_ = bf16[256,1024]{1,0:T(8,128)(2,1)S(1)} collective-permute-done((bf16[256,1024]{1,0:T(8,128)(2,1)S(1)}, bf16[256,1024]{1,0:T(8,128)(2,1)S(1)}, u32[]{:S(2)}, u32[]{:S(2)}) %collective-permute-start.8) | collective-permute-done | bytes 524320 | tf_op jit(solution)/shard_map/ppermute | solution.py:167
  132.1 1.6 %attend_6.1 = (bf16[128,4096]{1,0:T(8,128)(2,1)S(1)}, bf16[128,4096]{1,0:T(8,128)(2,1)S(1)}) custom-call(s32[8]{0:T(128)S(1)} %compare_select_fusion.10.refs_0_, bf16[128,8192]{1,0:T(8,128)(2,1)S(1)} %copy-done, bf16[128,4096]{1,0:T(8,128)(2,1)S(1)} %collective-permute-done.refs_2_, s32[256,128]{1,0:T(8,128)S(1)} %broadcast_in_dim.84.refs_3_, ...), custom_call_target="tpu_custom_call" | custom-call | flops 1073741824 | bytes 4194304 | tf_op jit(solution)/shard_map/attend_6/pallas_call | solution.py:143
  133.7 1.9 %collective-permute-start.10 = (bf16[128,4096]{1,0:T(8,128)(2,1)S(1)}, bf16[128,4096]{1,0:T(8,128)(2,1)S(1)}, u32[]{:S(2)}, u32[]{:S(2)}) collective-permute-start(bf16[128,4096]{1,0:T(8,128)(2,1)S(1)} %get-tuple-element.44), channel_id=1, source_target_pairs={{0,32},{32,0},{64,96},{96,64},{128,160},{160,128},{192,224},{224,1... | collective-permute-start | bytes 3145736 | tf_op jit(solution)/shard_map/ppermute | solution.py:170
  135.5 2.3 %collective-permute-done.10 = bf16[128,4096]{1,0:T(8,128)(2,1)S(1)} collective-permute-done((bf16[128,4096]{1,0:T(8,128)(2,1)S(1)}, bf16[128,4096]{1,0:T(8,128)(2,1)S(1)}, u32[]{:S(2)}, u32[]{:S(2)}) %collective-permute-start.10) | collective-permute-done | bytes 1048608 | tf_op jit(solution)/shard_map/ppermute | solution.py:170
  137.8 1.8 %maximum_select_fusion = bf16[128,8192]{1,0:T(8,128)(2,1)} fusion(bf16[128,4096]{1,0:T(8,128)(2,1)S(1)} %collective-permute-done.10, bf16[128,4096]{1,0:T(8,128)(2,1)S(1)} %get-tuple-element.43, pred[]{:T(512)S(6)} %eq.36), kind=kLoop, calls=%fused_computation | loop fusion | flops 9437184 | bytes 4194305 | tf_op jit(solution)/shard_map/jit(_where)/select_n | solution.py:235
  (3 shorter events, 0.0 us)
Async XLA Ops:
  0.0 43.5 %copy-start = (bf16[128,8192]{1,0:T(8,128)(2,1)S(1)}, bf16[128,8192]{1,0:T(8,128)(2,1)}, u32[]{:S(2)}) copy-start(bf16[128,8192]{1,0:T(8,128)(2,1)} %refs_1_.9) | copy-start | bytes 6291460
  0.0 5.4 %copy-start.1 = (s32[32]{0:T(128)S(1)}, s32[32]{0:T(128)}, u32[]{:S(2)}) copy-start(s32[32]{0:T(128)} %param.7) | copy-start | bytes 388
  2.8 40.6 %collective-permute-start = (bf16[128,4096]{1,0:T(8,128)(2,1)}, bf16[128,4096]{1,0:T(8,128)(2,1)S(1)}, u32[]{:S(2)}, u32[]{:S(2)}) collective-permute-start(bf16[128,4096]{1,0:T(8,128)(2,1)} %slice_select_fusion), channel_id=1, source_target_pairs={{0,32},{32,0},{64,96},{96,64},{128,160},{160,128},{192,224},{224,1... | collective-permute-start | bytes 3145736 | tf_op jit(solution)/shard_map/ppermute | solution.py:170
  5.4 1.9 %collective-permute-start.1 = (bf16[128,1024]{1,0:T(8,128)(2,1)}, bf16[128,1024]{1,0:T(8,128)(2,1)}, u32[]{:S(2)}, u32[]{:S(2)}) collective-permute-start(bf16[128,1024]{1,0:T(8,128)(2,1)} %get-tuple-element.46), channel_id=1, source_target_pairs={{0,32},{32,0},{64,96},{96,64},{128,160},{160,128},{192,224},{224,1... | collective-permute-start | bytes 786440 | tf_op jit(solution)/shard_map/ppermute | solution.py:170
  8.5 17.6 %collective-permute-start.3 = (bf16[256,1024]{1,0:T(8,128)(2,1)S(1)}, bf16[256,1024]{1,0:T(8,128)(2,1)S(1)}, u32[]{:S(2)}, u32[]{:S(2)}) collective-permute-start(bf16[256,1024]{1,0:T(8,128)(2,1)S(1)} %maximum_select_fusion.1.refs_4_), channel_id=1, source_target_pairs={{0,1},{32,33},{64,65},{96,97},{128,129},{160,161},{192,193},{224,2... | collective-permute-start | bytes 1572872 | tf_op jit(solution)/shard_map/ppermute | solution.py:167
  10.0 60.4 %collective-permute-start.2 = (bf16[256,1024]{1,0:T(8,128)(2,1)S(1)}, bf16[256,1024]{1,0:T(8,128)(2,1)S(1)}, u32[]{:S(2)}, u32[]{:S(2)}) collective-permute-start(bf16[256,1024]{1,0:T(8,128)(2,1)S(1)} %maximum_select_fusion.1.refs_4_), channel_id=1, source_target_pairs={{0,64},{32,96},{64,128},{96,160},{128,192},{160,224},{192,1},{224,... | collective-permute-start | bytes 1572872 | tf_op jit(solution)/shard_map/ppermute | solution.py:167
  13.1 57.3 %collective-permute-start.6 = (bf16[256,1024]{1,0:T(8,128)(2,1)S(1)}, bf16[256,1024]{1,0:T(8,128)(2,1)S(1)}, u32[]{:S(2)}, u32[]{:S(2)}) collective-permute-start(bf16[256,1024]{1,0:T(8,128)(2,1)S(1)} %maximum_select_fusion.1.refs_4_), channel_id=1, source_target_pairs={{0,2},{32,34},{64,66},{96,98},{128,130},{160,162},{192,194},{224,2... | collective-permute-start | bytes 1572872 | tf_op jit(solution)/shard_map/ppermute | solution.py:167
  26.2 54.0 %collective-permute-start.5 = (bf16[256,1024]{1,0:T(8,128)(2,1)S(1)}, bf16[256,1024]{1,0:T(8,128)(2,1)S(1)}, u32[]{:S(2)}, u32[]{:S(2)}) collective-permute-start(bf16[256,1024]{1,0:T(8,128)(2,1)S(1)} %collective-permute-done.3.refs_5_), channel_id=1, source_target_pairs={{0,223},{32,255},{64,0},{96,32},{128,64},{160,96},{192,128},{224,1... | collective-permute-start | bytes 1572872 | tf_op jit(solution)/shard_map/ppermute | solution.py:167
  70.4 16.8 %collective-permute-start.7 = (bf16[256,1024]{1,0:T(8,128)(2,1)S(1)}, bf16[256,1024]{1,0:T(8,128)(2,1)S(1)}, u32[]{:S(2)}, u32[]{:S(2)}) collective-permute-start(bf16[256,1024]{1,0:T(8,128)(2,1)S(1)} %collective-permute-done.2.refs_4_), channel_id=1, source_target_pairs={{0,1},{32,33},{64,65},{96,97},{128,129},{160,161},{192,193},{224,2... | collective-permute-start | bytes 1572872 | tf_op jit(solution)/shard_map/ppermute | solution.py:167
  70.4 43.5 %collective-permute-start.4 = (bf16[256,1024]{1,0:T(8,128)(2,1)S(1)}, bf16[256,1024]{1,0:T(8,128)(2,1)S(1)}, u32[]{:S(2)}, u32[]{:S(2)}) collective-permute-start(bf16[256,1024]{1,0:T(8,128)(2,1)S(1)} %collective-permute-done.2.refs_4_), channel_id=1, source_target_pairs={{0,64},{32,96},{64,128},{96,160},{128,192},{160,224},{192,1},{224,... | collective-permute-start | bytes 1572872 | tf_op jit(solution)/shard_map/ppermute | solution.py:167
  80.2 40.0 %collective-permute-start.9 = (bf16[256,1024]{1,0:T(8,128)(2,1)S(1)}, bf16[256,1024]{1,0:T(8,128)(2,1)S(1)}, u32[]{:S(2)}, u32[]{:S(2)}) collective-permute-start(bf16[256,1024]{1,0:T(8,128)(2,1)S(1)} %collective-permute-done.5.refs_4_), channel_id=1, source_target_pairs={{0,1},{32,33},{64,65},{96,97},{128,129},{160,161},{192,193},{224,2... | collective-permute-start | bytes 1572872 | tf_op jit(solution)/shard_map/ppermute | solution.py:167
  113.9 18.2 %collective-permute-start.8 = (bf16[256,1024]{1,0:T(8,128)(2,1)S(1)}, bf16[256,1024]{1,0:T(8,128)(2,1)S(1)}, u32[]{:S(2)}, u32[]{:S(2)}) collective-permute-start(bf16[256,1024]{1,0:T(8,128)(2,1)S(1)} %collective-permute-done.4.refs_4_), channel_id=1, source_target_pairs={{0,1},{32,33},{64,65},{96,97},{128,129},{160,161},{192,193},{224,2... | collective-permute-start | bytes 1572872 | tf_op jit(solution)/shard_map/ppermute | solution.py:167
  133.7 4.2 %collective-permute-start.10 = (bf16[128,4096]{1,0:T(8,128)(2,1)S(1)}, bf16[128,4096]{1,0:T(8,128)(2,1)S(1)}, u32[]{:S(2)}, u32[]{:S(2)}) collective-permute-start(bf16[128,4096]{1,0:T(8,128)(2,1)S(1)} %get-tuple-element.44), channel_id=1, source_target_pairs={{0,32},{32,0},{64,96},{96,64},{128,160},{160,128},{192,224},{224,1... | collective-permute-start | bytes 3145736 | tf_op jit(solution)/shard_map/ppermute | solution.py:170
